TPU v7x, 128 devices: a whole 4x4x4 slice. The times are simulated.
128 devices in a mesh: rep: 2 (over core), dp: 64 (over x, y, z).
Axes of the slice: x: 4, y: 4, z: 4, core: 2. Of those that a mesh axis runs over, the one named last changes fastest.
Arguments:
- x: bfloat16 [128, 2048, 1024], P(('rep', 'dp')), parts along dimension 0
- dy: bfloat16 [128, 2048, 1024], P(('rep', 'dp')), parts along dimension 0
- w_gate: bfloat16 [2, 1024, 3200], replicated
- w_up: bfloat16 [2, 1024, 3200], replicated
- w_down: bfloat16 [2, 3200, 1024], replicated
- m_w_gate: float32 [2, 1024, 3200], replicated
- m_w_up: float32 [2, 1024, 3200], replicated
- m_w_down: float32 [2, 3200, 1024], replicated
- v_w_gate: float32 [2, 1024, 3200], replicated
- v_w_up: float32 [2, 1024, 3200], replicated
- v_w_down: float32 [2, 3200, 1024], replicated
Outputs:
- output 1: bfloat16 [4, 1024, 3200], P('rep'), parts along dimension 0
- output 2: bfloat16 [4, 1024, 3200], P('rep'), parts along dimension 0
- output 3: bfloat16 [4, 3200, 1024], P('rep'), parts along dimension 0
- output 4: float32 [4, 1024, 3200], P('rep'), parts along dimension 0
- output 5: float32 [4, 1024, 3200], P('rep'), parts along dimension 0
- output 6: float32 [4, 3200, 1024], P('rep'), parts along dimension 0
- output 7: float32 [4, 1024, 3200], P('rep'), parts along dimension 0
- output 8: float32 [4, 1024, 3200], P('rep'), parts along dimension 0
- output 9: float32 [4, 3200, 1024], P('rep'), parts along dimension 0
There are 2 independent parts. A program takes and returns all parts, laid end to end along the dimension named above; an argument that names none is the same for every part.
All inputs are finite; a program needn't handle non-finite values.
Results may differ from a plain program's by a relative error of at most 0.022.
Values are sent between devices in bfloat16 or wider.
A program may use at most 1.5 GiB of HBM per device.

v0:
```python
import jax
import jax.numpy as jnp
from jax import lax
from jax.sharding import PartitionSpec as P

NAMES = ("w_gate", "w_up", "w_down")


def matmul(a, w):
    return jnp.dot(a, w, preferred_element_type=jnp.float32).astype(jnp.bfloat16)


def normed(h):
    wide = h.astype(jnp.float32)
    scale = lax.rsqrt(jnp.mean(wide**2, -1, keepdims=True) + 1e-6)
    return (wide * scale).astype(jnp.bfloat16)


def layer(h, w):
    a = normed(h)
    gate = jnp.dot(a, w["w_gate"], preferred_element_type=jnp.float32)
    up = jnp.dot(a, w["w_up"], preferred_element_type=jnp.float32)
    return h + matmul((jax.nn.silu(gate) * up).astype(jnp.bfloat16), w["w_down"])


def adamw(w, m, v, g):
    m = 0.9 * m + 0.1 * g
    v = 0.95 * v + 0.05 * g * g
    step = m * lax.rsqrt(v + 1e-8) + 0.1 * w
    return (w - 0.02 * step).astype(jnp.bfloat16), m, v


def solution(mesh):
    def step(x, dy, *arrays):
        weights, m, v = (arrays[i : i + 3] for i in (0, 3, 6))
        layers = weights[0].shape[0]
        h, kept = x[0], []
        for number in range(layers):
            kept.append(h)
            h = layer(h, {name: w[number] for name, w in zip(NAMES, weights, strict=True)})
        by_h, summed = dy[0], [None] * layers
        for number in reversed(range(layers)):
            _, back = jax.vjp(lambda w, h: layer(h, w), {name: w[number] for name, w in zip(NAMES, weights, strict=True)}, kept[number])
            by_w, by_h = back(by_h)
            summed[number] = [lax.psum(by_w[name], "dp") for name in NAMES]
        gradients = [jnp.stack([summed[number][i] for number in range(layers)]).astype(jnp.float32) for i in range(3)]
        new = [adamw(w.astype(jnp.float32), m, v, g) for w, m, v, g in zip(weights, m, v, gradients, strict=True)]
        return tuple(one[which] for which in range(3) for one in new)

    return jax.shard_map(
        step,
        mesh=mesh,
        in_specs=(P(("rep", "dp"), None, None),) * 2 + (P(None, None, None),) * 9,
        out_specs=(P("rep", None, None),) * 9,
        check_vma=False,
    )
```

profile of v0, /device:TPU:1, one launch (start us, length us, event | category | flops | bytes accessed | tf_op | source)
XLA Modules:
  0.0 918.1 jit_solution(759406642165531524)
XLA Ops:
  7.2 0.0 all-reduce.3.cloned.1.call-start
  7.2 6.5 copy.20
  13.7 3.1 fusion.30
  16.8 6.5 copy.21
  23.3 20.9 %convolution_convert_fusion.1 = bf16[2048,3200]{1,0:T(8,128)(2,1)} fusion(bf16[2,3200,1024]{2,1,0:T(8,128)(2,1)} %param.15, bf16[1,2048,1024]{2,1,0:T(8,128)(2,1)} %param.12), kind=kOutput, calls=%fused_computation.50 | convolution fusion | flops 13428326400 | bytes 23855104 | tf_op jit(solution)/shard_map/transpose(jvp())/dot_general | solution.py:10
  44.2 0.0 copy-done.3
  44.2 20.9 %fusion.56 = f32[2048,3200]{1,0:T(8,128)} fusion(bf16[2,1024,3200]{2,1,0:T(8,128)(2,1)} %param.13, bf16[1,2048,1024]{2,1,0:T(8,128)(2,1)S(1)} %copy-done.3, f32[2048]{0:T(1024)S(1)} %add_rsqrt_fusion), kind=kOutput, calls=%fused_computation.90 | convolution fusion | flops 13428064256 | bytes 36970496 | tf_op jit(solution)/shard_map/dot_general | solution.py:21
  65.1 0.0 copy-done.6
  65.1 32.4 %multiply_convert_fusion.1 = (bf16[2048,3200]{1,0:T(8,128)(2,1)}, f32[2048,3200]{1,0:T(8,128)}) fusion(f32[2048,3200]{1,0:T(8,128)} %fusion.56, bf16[2,1024,3200]{2,1,0:T(8,128)(2,1)} %param.14, bf16[1,2048,1024]{2,1,0:T(8,128)(2,1)} %param.11, f32[2048]{0:T(1024)S(1)} %add_rsqrt_fusion), kind=kOutput, calls=%fused_computation.44 | convolution fusion | flops 13467385856 | bytes 76292096 | tf_op jit(solution)/shard_map/dot_general | solution.py:22
  97.6 21.9 %fusion.34 = (f32[2048]{0:T(1024)S(1)}, bf16[2048,1024]{0,1:T(8,128)(2,1)}) fusion(bf16[2048,3200]{1,0:T(8,128)(2,1)} %get-tuple-element.24, bf16[2,3200,1024]{2,1,0:T(8,128)(2,1)} %param.15, bf16[1,2048,1024]{1,2,0:T(8,128)(2,1)} %copy.20), kind=kOutput, calls=%fused_computation.67 | convolution fusion | flops 13432256512 | bytes 28057600 | tf_op jit(solution)/shard_map/dot_general | solution.py:10
  119.4 23.3 %fusion.43 = f32[2048,3200]{1,0:T(8,128)} fusion(bf16[2,1024,3200]{2,1,0:T(8,128)(2,1)} %param.14, bf16[2048,1024]{0,1:T(8,128)(2,1)} %get-tuple-element.27, f32[2048]{0:T(1024)S(1)} %fusion.92), kind=kOutput, calls=%fused_computation.77 | convolution fusion | flops 13428064256 | bytes 36970496 | tf_op jit(solution)/shard_map/jvp()/dot_general | solution.py:22
  142.8 0.0 copy-done.4
  142.8 38.9 %fusion.14 = (bf16[2048,3200]{1,0:T(8,128)(2,1)}, f32[2048,3200]{1,0:T(8,128)}) fusion(f32[2048,3200]{1,0:T(8,128)} %fusion.43, bf16[2048,3200]{1,0:T(8,128)(2,1)} %convolution_convert_fusion.1, bf16[2,1024,3200]{2,1,0:T(8,128)(2,1)} %param.13, bf16[2048,1024]{0,1:T(8,128)(2,1)} %get-tuple-element.27, f32[2048]{0:T(1024)S(1)} %fusion.92), kind=kOutput, calls=%fused_computation.32 | convolution fusion | flops 13506707456 | bytes 89399296 | tf_op jit(solution)/shard_map/jvp()/dot_general | solution.py:21
  181.7 22.6 %fusion.27 = bf16[2048,1024]{0,1:T(8,128)(2,1)} fusion(bf16[2048,3200]{1,0:T(8,128)(2,1)} %convolution_convert_fusion.1, bf16[2,1024,3200]{2,1,0:T(8,128)(2,1)} %param.14, f32[2048,3200]{1,0:T(8,128)} %get-tuple-element.29), kind=kOutput, calls=%fused_computation.48 | convolution fusion | flops 13461094400 | bytes 50069504 | tf_op jit(solution)/shard_map/transpose(jvp())/dot_general | solution.py:22
  204.3 0.0 copy-done.2
  204.3 24.2 %fusion.64 = bf16[1,1024,3200]{2,1,0:T(8,128)(2,1)} fusion(bf16[2048,3200]{1,0:T(8,128)(2,1)} %convolution_convert_fusion.1, bf16[2048,1024]{0,1:T(8,128)(2,1)S(1)} %copy-done.2, f32[2048]{0:T(1024)S(1)} %fusion.92, f32[2048,3200]{1,0:T(8,128)} %get-tuple-element.29), kind=kOutput, calls=%fused_computation.98 | convolution fusion | flops 13470662656 | bytes 50077696 | tf_op jit(solution)/shard_map/transpose(jvp())/dot_general | solution.py:22
  228.5 25.9 %fusion.65 = bf16[1,3200,1024]{2,1,0:T(8,128)(2,1)} fusion(f32[2048,3200]{1,0:T(8,128)} %fusion.43, bf16[1,2048,1024]{2,1,0:T(8,128)(2,1)} %param.12, f32[2048,3200]{1,0:T(8,128)} %get-tuple-element.29), kind=kOutput, calls=%fused_computation.99 | convolution fusion | flops 13464371200 | bytes 63176704 | tf_op jit(solution)/shard_map/transpose(jvp())/dot_general | solution.py:10
  254.4 21.2 %fusion.61 = bf16[1,1024,3200]{2,1,0:T(8,128)(2,1)} fusion(bf16[2048,3200]{1,0:T(8,128)(2,1)} %get-tuple-element.28, bf16[2048,1024]{0,1:T(8,128)(2,1)} %get-tuple-element.27, f32[2048]{0:T(1024)S(1)} %fusion.92), kind=kOutput, calls=%fused_computation.95 | convolution fusion | flops 13428064256 | bytes 23863296 | tf_op jit(solution)/shard_map/transpose(jvp())/dot_general | solution.py:21
  275.6 22.8 %fusion.36 = (f32[2048]{0:T(1024)S(1)}, bf16[2048,1024]{0,1:T(8,128)(2,1)}) fusion(bf16[2048,1024]{0,1:T(8,128)(2,1)} %get-tuple-element.27, bf16[2048,1024]{0,1:T(8,128)(2,1)} %fusion.27, bf16[2048,3200]{1,0:T(8,128)(2,1)} %get-tuple-element.28, bf16[2,1024,3200]{2,1,0:T(8,128)(2,1)} %param.13), kind=kOutput, calls=%fused_computation.69 | convolution fusion | flops 13432256512 | bytes 32251904 | tf_op jit(solution)/shard_map/transpose(jvp())/dot_general | solution.py:21
  298.4 0.0 copy-done.5
  298.4 0.0 copy-done
  298.4 6.6 fusion.77
  305.1 21.1 %convolution_convert_fusion = bf16[2048,3200]{1,0:T(8,128)(2,1)} fusion(bf16[2048,1024]{0,1:T(8,128)(2,1)} %fusion.77, bf16[2,3200,1024]{2,1,0:T(8,128)(2,1)} %param.15), kind=kOutput, calls=%fused_computation.49 | convolution fusion | flops 13428326400 | bytes 23855104 | tf_op jit(solution)/shard_map/transpose(jvp())/dot_general | solution.py:10
  326.2 21.2 %fusion.62 = bf16[1,3200,1024]{2,1,0:T(8,128)(2,1)} fusion(bf16[2048,3200]{1,0:T(8,128)(2,1)} %get-tuple-element.24, bf16[2048,1024]{0,1:T(8,128)(2,1)} %fusion.77), kind=kOutput, calls=%fused_computation.96 | convolution fusion | flops 13425049600 | bytes 23855104 | tf_op jit(solution)/shard_map/transpose(jvp())/dot_general | solution.py:10
  347.4 0.0 copy-done.1
  347.4 0.0 copy-done.7
  347.4 24.2 %fusion.63 = bf16[1,1024,3200]{2,1,0:T(8,128)(2,1)} fusion(bf16[2048,3200]{1,0:T(8,128)(2,1)} %convolution_convert_fusion, f32[2048,3200]{1,0:T(8,128)} %fusion.56, bf16[1,2048,1024]{1,2,0:T(8,128)(2,1)S(1)} %copy-done.1, f32[2048]{0:T(1024)S(1)} %copy-done.7), kind=kOutput, calls=%fused_computation.97 | convolution fusion | flops 13470662656 | bytes 50077696 | tf_op jit(solution)/shard_map/transpose(jvp())/dot_general | solution.py:22
  371.5 29.6 %fusion.66 = bf16[1,1024,3200]{2,1,0:T(8,128)(2,1)} fusion(f32[2048,3200]{1,0:T(8,128)} %fusion.56, f32[2048,3200]{1,0:T(8,128)} %get-tuple-element.25, bf16[2048,3200]{1,0:T(8,128)(2,1)} %convolution_convert_fusion, bf16[1,2048,1024]{1,2,0:T(8,128)(2,1)S(1)} %copy-done.1, f32[2048]{0:T(1024)S(1)} %copy-done.7), kind=kOutput, calls=%fused_computation.100 | convolution fusion | flops 13503430656 | bytes 76292096 | tf_op jit(solution)/shard_map/transpose(jvp())/dot_general | solution.py:21
  401.2 0.0 all-reduce.3.cloned.1.call-update
  401.2 368.5 %all-reduce.3.cloned.1.call-done = (bf16[1,1024,3200]{2,1,0:T(8,128)(2,1)}, bf16[1,1024,3200]{2,1,0:T(8,128)(2,1)}, bf16[1,1024,3200]{2,1,0:T(8,128)(2,1)}, bf16...) async-done(((bf16[1,1024,3200]{2,1,0:T(8,128)(2,1)}, bf16[1,1024,3200]{2,1,0:T(8,128)(2,1)}, ...) | async-done | bytes 39321616 | tf_op jit(solution)/shard_map/psum | solution.py:45
  769.7 49.7 %fusion.11 = (bf16[2,3200,1024]{2,1,0:T(8,128)(2,1)}, f32[2,3200,1024]{2,1,0:T(8,128)}, f32[2,3200,1024]{2,1,0:T(8,128)}) fusion(bf16[2,3200,1024]{2,1,0:T(8,128)(2,1)} %param.15, bf16[1,3200,1024]{2,1,0:T(8,128)(2,1)} %get-tuple-element.13, bf16[1,3200,1024]{2,1,0:T(8,128)(2,1)} %get-tuple-element.14, f32[2,3200,1024]{2,1,0:T(8,128)} %param.21, ...), kind=kLoop, calls=%fused_computation.29 | loop fusion | flops 124518400 | bytes 144179200 | tf_op jit(solution)/shard_map/convert_element_type | solution.py:30
  819.4 91.6 %fusion.2 = (bf16[2,1024,3200]{2,1,0:T(8,128)(2,1)}, f32[2,1024,3200]{2,1,0:T(8,128)}, f32[2,1024,3200]{2,1,0:T(8,128)}, bf16[2,1024,3200]{2,1,0:T(8,128)(2,1)},...) fusion(bf16[2,1024,3200]{2,1,0:T(8,128)(2,1)} %param.13, bf16[1,1024,3200]{2,1,0:T(8,128)(2,1)} %get-tuple-element.9, ...), kind=kLoop, calls=%fused_computation.20 | loop fusion | flops 249036800 | bytes 288358400 | tf_op jit(solution)/shard_map/convert_element_type | solution.py:30
  (11 shorter events, 0.0 us)
Async XLA Ops:
  7.2 762.5 %all-reduce.3.cloned.1.call-start = ((), (), s32[]{:S(2)}) async-start(), calls=%async_computation | async-start | bytes 78643200 | tf_op jit(solution)/shard_map/psum | solution.py:45
  16.8 48.3 %copy-start.6 = (f32[2048]{0:T(1024)}, f32[2048]{0:T(1024)S(1)}, u32[]{:S(2)}) copy-start(f32[2048]{0:T(1024)S(1)} %add_rsqrt_fusion) | copy-start | bytes 24580
  23.3 20.9 %copy-start.3 = (bf16[1,2048,1024]{2,1,0:T(8,128)(2,1)S(1)}, bf16[1,2048,1024]{2,1,0:T(8,128)(2,1)}, u32[]{:S(2)}) copy-start(bf16[1,2048,1024]{2,1,0:T(8,128)(2,1)} %param.11) | copy-start | bytes 12582916
  119.4 23.3 %copy-start.4 = (f32[2048]{0:T(1024)}, f32[2048]{0:T(1024)S(1)}, u32[]{:S(2)}) copy-start(f32[2048]{0:T(1024)S(1)} %get-tuple-element.26) | copy-start | bytes 24580
  181.7 22.6 %copy-start.2 = (bf16[2048,1024]{0,1:T(8,128)(2,1)S(1)}, bf16[2048,1024]{0,1:T(8,128)(2,1)}, u32[]{:S(2)}) copy-start(bf16[2048,1024]{0,1:T(8,128)(2,1)} %get-tuple-element.27) | copy-start | bytes 12582916
  275.6 22.8 %copy-start.5 = (f32[2048]{0:T(1024)S(1)}, f32[2048]{0:T(1024)}, u32[]{:S(2)}) copy-start(f32[2048]{0:T(1024)} %copy-done.4) | copy-start | bytes 24580
  275.6 22.8 %copy-start = (bf16[1,2048,1024]{1,2,0:T(8,128)(2,1)S(1)}, bf16[1,2048,1024]{1,2,0:T(8,128)(2,1)}, u32[]{:S(2)}) copy-start(bf16[1,2048,1024]{1,2,0:T(8,128)(2,1)} %copy.21) | copy-start | bytes 12582916
  326.2 21.2 %copy-start.1 = (bf16[1,2048,1024]{1,2,0:T(8,128)(2,1)S(1)}, bf16[1,2048,1024]{1,2,0:T(8,128)(2,1)}, u32[]{:S(2)}) copy-start(bf16[1,2048,1024]{1,2,0:T(8,128)(2,1)} %copy.20) | copy-start | bytes 12582916
  326.2 21.2 %copy-start.7 = (f32[2048]{0:T(1024)S(1)}, f32[2048]{0:T(1024)}, u32[]{:S(2)}) copy-start(f32[2048]{0:T(1024)} %copy-done.6) | copy-start | bytes 24580
Sparse Core Ops, SparseCore 0:
  401.3 368.3 all-reduce.2
where the time goes:
time: 926 us; the launch traced here: 918 us
  matrix products  371 us (40%)
  waiting for transfers between devices  369 us (40%)
  other arithmetic  151 us (16%)
  between operations  14.3 us (2%)
  local copies, waits for them, and re-layouts  13 us (1%)
    psum x1, waiting for transfers between devices, step(): summed[number] = [lax.psum(by_w[name], 'dp') for name in NAMES]  369 us
    convert_element_type x2, other arithmetic, adamw(): return ((w - 0.02 * step).astype(jnp.bfloat16), m, v)  141 us
    dot_general x5, matrix products, layer(): gate = jnp.dot(a, w['w_gate'], preferred_element_type=jnp.float32)  133 us
    dot_general x5, matrix products, layer(): up = jnp.dot(a, w['w_up'], preferred_element_type=jnp.float32)  127 us
    dot_general x5, matrix products, matmul(): jnp.dot(a, w, preferred_element_type=jnp.float32).astype(jnp.bfloat16)  111 us
  transfers between devices with their start and end apart: 1, of which 1 were waited for; matrix products, arithmetic and copies ran while one was open for 0% of the time, Pallas kernels for 0%

commit v1 on v0

v1 whole, which is shorter than its diff:
```python
import functools
import jax
import jax.numpy as jnp
from jax import lax
from jax.experimental import pallas as pl
from jax.experimental.pallas import tpu as pltpu
from jax.sharding import PartitionSpec as P

F32, BF = jnp.float32, jnp.bfloat16
TILE = 512

def vmem(mib):
    return pltpu.CompilerParams(vmem_limit_bytes=mib << 20, dimension_semantics=("arbitrary",))

def cost(flops, nbytes):
    return pl.CostEstimate(flops=flops, bytes_accessed=nbytes, transcendentals=0)

def nn(a, b):
    return lax.dot_general(a, b, (((1,), (0,)), ((), ())), preferred_element_type=F32)

def nt(a, b):
    return lax.dot_general(a, b, (((1,), (1,)), ((), ())), preferred_element_type=F32)

def rows(i):
    return pl.ds(i * TILE, TILE)

def sig(x):
    return 1.0 / (1.0 + jnp.exp(-x))

def ready_kernel(x, dy, a, at, dyt):
    wide = x[...].astype(F32)
    n = wide * lax.rsqrt(jnp.mean(wide * wide, -1, keepdims=True) + 1e-6)
    a[...] = n.astype(BF)
    at[...] = n.astype(BF).T
    dyt[...] = dy[...].T

def ready(x, dy, block=256):
    t, d = x.shape
    tok = pl.BlockSpec((block, d), lambda i: (i, 0))
    tokt = pl.BlockSpec((d, block), lambda i: (0, i))
    return pl.pallas_call(
        ready_kernel, grid=(t // block,), in_specs=[tok, tok], out_specs=[tok, tokt, tokt],
        out_shape=[jax.ShapeDtypeStruct((t, d), BF)] + [jax.ShapeDtypeStruct((d, t), BF)] * 2,
        compiler_params=vmem(60), name="ready", cost_estimate=cost(10 * t * d, 10 * t * d),
    )(x, dy)

def gated_kernel(a, wg, wu, act, gate, up):
    for i in range(a.shape[0] // TILE):
        g, u = nn(a[rows(i)], wg[0]), nn(a[rows(i)], wu[0])
        gate[rows(i)] = g
        up[rows(i)] = u
        act[rows(i)] = (g * sig(g) * u).astype(BF)

def gated(a, w_gate, w_up, number, block=256):
    t, d = a.shape
    ff = w_gate.shape[2]
    whole = pl.BlockSpec((t, d), lambda j: (0, 0))
    w = pl.BlockSpec((1, d, block), lambda j: (number, 0, j))
    out = pl.BlockSpec((t, block), lambda j: (0, j))
    return pl.pallas_call(
        gated_kernel, grid=(pl.cdiv(ff, block),), in_specs=[whole, w, w], out_specs=[out] * 3,
        out_shape=[jax.ShapeDtypeStruct((t, ff), x) for x in (BF, F32, F32)],
        compiler_params=vmem(60), name="gated", cost_estimate=cost(4 * t * d * ff, 10 * t * ff + 4 * d * ff),
    )(a, w_gate, w_up)

def down_kernel(act, w, h, out, a, at):
    o = h[...].astype(F32) + nn(act[...], w[0]).astype(BF).astype(F32)
    o = o.astype(BF)
    out[...] = o
    wide = o.astype(F32)
    scale = lax.rsqrt(jnp.mean(wide * wide, -1, keepdims=True) + 1e-6)
    n = wide * scale
    a[...] = n.astype(BF)
    at[...] = n.astype(BF).T

def down(act, w_down, h, number, block=512):
    t, d = h.shape
    ff = act.shape[1]
    tok = pl.BlockSpec((block, d), lambda i: (i, 0))
    return pl.pallas_call(
        down_kernel, grid=(t // block,),
        in_specs=[pl.BlockSpec((block, ff), lambda i: (i, 0)), pl.BlockSpec((1, ff, d), lambda i: (number, 0, 0)), tok],
        out_specs=[tok, tok, pl.BlockSpec((d, block), lambda i: (0, i))],
        out_shape=[jax.ShapeDtypeStruct((t, d), BF)] * 2 + [jax.ShapeDtypeStruct((d, t), BF)],
        compiler_params=vmem(60), name="down", cost_estimate=cost(2 * t * d * ff, 2 * t * ff + 2 * d * ff),
    )(act, w_down, h)

def split(g, u, da):
    s = sig(g)
    silu = g * s
    return (silu * u), da * u * (s + silu * (1.0 - s)), da * silu

LAG = 2
STAGES = 5
STRIDE = (16, 4, 1)


def exchange_scratch(units, block):
    local, kept = 2 * LAG + 1, LAG + 1
    return [
        pltpu.VMEM((3, local, 1152, block), BF),
        pltpu.VMEM((3, units, 2, 256, block), BF),
        pltpu.VMEM((3, units, 2, 128, block), BF),
        pltpu.VMEM((3, local, 256, block), F32),
        pltpu.VMEM((3, kept, 288, block), BF),
        pltpu.VMEM((3, units, 2, 64, block), BF),
        pltpu.VMEM((3, units, 2, 32, block), BF),
        pltpu.VMEM((3, kept, 64, block), F32),
        pltpu.VMEM((3, kept, 64, block), BF),
        pltpu.VMEM((3, units, 3, 16, block), BF),
        pltpu.SemaphoreType.DMA((3, kept, 11)),
        pltpu.SemaphoreType.DMA((3, units, 11)),
    ]


def steps_of(units):
    return units + 1 + STAGES * LAG


def exchange(k, units, out, scratch):
    term, in0, in1, one, one_b, in2, in3, two, two_b, in4, sent, got = scratch
    local, kept = 2 * LAG + 1, LAG + 1
    me = lax.axis_index("dp")
    at = (lax.div(me, 16), lax.rem(lax.div(me, 4), 4), lax.rem(me, 4))

    def near(dim, by):
        return lax.rem(at[dim] + by, 4)

    def peer(dim, by):
        return me + (near(dim, by) - at[dim]) * STRIDE[dim]

    def rows(start, n, step=None):
        return pl.ds(pl.multiple_of(start, step or min(n, 128)), n)

    @pl.when(k == 0)
    def _():
        barrier = pltpu.get_barrier_semaphore()
        for dim in range(3):
            for by in (1, 2, 3):
                pl.semaphore_signal(barrier, inc=1, device_id={"dp": peer(dim, by)}, device_id_type=pl.DeviceIdType.MESH)
        pl.semaphore_wait(barrier, 9)

    def copies(stage, u):
        made = []
        lu, ku = lax.rem(u, local), lax.rem(u, kept)

        def add(c, i, src, dst, dim, by):
            made.append(
                pltpu.make_async_remote_copy(
                    src_ref=src, dst_ref=dst, send_sem=sent.at[c, ku, i], recv_sem=got.at[c, u, i],
                    device_id={"dp": peer(dim, by)}, device_id_type=pl.DeviceIdType.MESH,
                )
            )

        for c in range(3):
            d1, d2, d3 = c, (c + 1) % 3, (c + 2) % 3
            if stage == 0:
                add(c, 0, term.at[c, lu, rows(near(d1, 1) * 256 + 128, 256)], in0.at[c, u, 0], d1, 1)
                add(c, 1, term.at[c, lu, rows(near(d1, 2) * 256 + 128, 256)], in0.at[c, u, 1], d1, 3)
            if stage == 1:
                add(c, 2, in0.at[c, u, 0, pl.ds(128, 128)], in1.at[c, u, 0], d1, 1)
                add(c, 3, in0.at[c, u, 1, pl.ds(0, 128)], in1.at[c, u, 1], d1, 3)
            if stage == 2:
                add(c, 4, one_b.at[c, ku, rows(near(d2, 1) * 64 + 32, 64, 32)], in2.at[c, u, 0], d2, 1)
                add(c, 5, one_b.at[c, ku, rows(near(d2, 2) * 64 + 32, 64, 32)], in2.at[c, u, 1], d2, 3)
            if stage == 3:
                add(c, 6, in2.at[c, u, 0, pl.ds(32, 32)], in3.at[c, u, 0], d2, 1)
                add(c, 7, in2.at[c, u, 1, pl.ds(0, 32)], in3.at[c, u, 1], d2, 3)
            if stage == 4:
                for by in (1, 2, 3):
                    add(c, 7 + by, two_b.at[c, ku, rows(near(d3, by) * 16, 16)], in4.at[c, u, by - 1], d3, by)
        return made

    def wide(ref, c, u, r):
        return ref[c, u, r].astype(F32)

    def work(stage, u):
        lu, ku = lax.rem(u, local), lax.rem(u, kept)
        for c in range(3):
            d1, d2, d3 = c, (c + 1) % 3, (c + 2) % 3
            if stage == 1:
                s = in0[c, u, 0, pl.ds(128, 128)].astype(F32) + wide(term, c, lu, rows(near(d1, 1) * 256, 128))
                in0[c, u, 0, pl.ds(128, 128)] = s.astype(BF)
                s = in0[c, u, 1, pl.ds(0, 128)].astype(F32) + wide(term, c, lu, rows(near(d1, 3) * 256 + 128, 128))
                in0[c, u, 1, pl.ds(0, 128)] = s.astype(BF)
            if stage == 2:
                own = at[d1] * 256
                s = wide(term, c, lu, rows(own, 128)) + in0[c, u, 1, pl.ds(128, 128)].astype(F32) + in1[c, u, 0].astype(F32)
                one[c, lu, pl.ds(0, 128)] = s
                one_b[c, ku, pl.ds(0, 128)] = s.astype(BF)
                one_b[c, ku, pl.ds(256, 32)] = s[:32].astype(BF)
                s = wide(term, c, lu, rows(own + 128, 128)) + in0[c, u, 0, pl.ds(0, 128)].astype(F32) + in1[c, u, 1].astype(F32)
                one[c, lu, pl.ds(128, 128)] = s
                one_b[c, ku, pl.ds(128, 128)] = s.astype(BF)
            if stage == 3:
                s = in2[c, u, 0, pl.ds(32, 32)].astype(F32) + one[c, lu, rows(near(d2, 1) * 64, 32)]
                in2[c, u, 0, pl.ds(32, 32)] = s.astype(BF)
                s = in2[c, u, 1, pl.ds(0, 32)].astype(F32) + one[c, lu, rows(near(d2, 3) * 64 + 32, 32)]
                in2[c, u, 1, pl.ds(0, 32)] = s.astype(BF)
            if stage == 4:
                own = at[d2] * 64
                s = one[c, lu, rows(own, 32)] + in2[c, u, 1, pl.ds(32, 32)].astype(F32) + in3[c, u, 0].astype(F32)
                two[c, ku, pl.ds(0, 32)] = s
                two_b[c, ku, pl.ds(0, 32)] = s.astype(BF)
                s = one[c, lu, rows(own + 32, 32)] + in2[c, u, 0, pl.ds(0, 32)].astype(F32) + in3[c, u, 1].astype(F32)
                two[c, ku, pl.ds(32, 32)] = s
                two_b[c, ku, pl.ds(32, 32)] = s.astype(BF)
            if stage == 5:
                s = two[c, ku, rows(at[d3] * 16, 16)]
                for i in range(3):
                    s = s + in4[c, u, i].astype(F32)
                out[c] = s.astype(BF)

    for stage in range(STAGES + 1):
        u = k - 1 - stage * LAG

        @pl.when((u >= 0) & (u < units))
        def _(stage=stage, u=u):
            if stage:
                for copy in copies(stage - 1, u):
                    copy.wait()
                work(stage, u)
            if stage < STAGES:
                for copy in copies(stage, u):
                    copy.start()


def keep(term, c, slot, i, value):
    term[c, slot, pl.ds(i * TILE, TILE)] = value
    if i == 0:
        term[c, slot, pl.ds(1024, 128)] = value[:128]


def sums(k, units, scratch, pairs):
    for i in range(pairs[0][0].shape[0] // TILE):
        for c, (left, right) in enumerate(pairs):
            keep(scratch[0], c, lax.rem(k, 2 * LAG + 1), i, nn(left[rows(i)], right[...]).astype(BF))


def last_kernel(units, a, at, dy, dyt, wg, wu, wd, out, dg_out, du_out, act, *scratch):
    k = pl.program_id(0)
    exchange(k, units, out, scratch)

    @pl.when(k < units)
    def _():
        for i in range(a.shape[0] // TILE):
            g, u, da = nn(a[rows(i)], wg[0]), nn(a[rows(i)], wu[0]), nt(dy[rows(i)], wd[0]).astype(BF).astype(F32)
            c, dg, du = split(g, u, da)
            act[rows(i)] = c.astype(BF)
            dg_out[rows(i)] = dg.astype(BF)
            du_out[rows(i)] = du.astype(BF)
        sums(k, units, scratch, ((dyt, act), (at, dg_out), (at, du_out)))


def specs(t, d, units, block, number):
    def j(k):
        return jnp.minimum(k, units - 1)

    once = pl.Buffered(1)
    return (
        pl.BlockSpec((t, d), lambda k: (0, 0), pipeline_mode=once),
        pl.BlockSpec((d, t), lambda k: (0, 0), pipeline_mode=once),
        pl.BlockSpec((1, d, block), lambda k: (number, 0, j(k))),
        pl.BlockSpec((1, block, d), lambda k: (number, j(k), 0)),
        pl.BlockSpec((t, block), lambda k: (0, j(k))),
        pl.BlockSpec((3, 16, block), lambda k: (0, 0, jnp.clip(k - 1 - STAGES * LAG, 0, units - 1))),
    )


def sending(number):
    return pltpu.CompilerParams(vmem_limit_bytes=63 << 20, dimension_semantics=("arbitrary",), collective_id=number, has_side_effects=True)


def last(a, at, dy, dyt, w_gate, w_up, w_down, number, block=256):
    t, d = a.shape
    ff = w_gate.shape[2]
    units = pl.cdiv(ff, block)
    tok, tokt, w, wt, hid, out = specs(t, d, units, block, number)
    return pl.pallas_call(
        functools.partial(last_kernel, units), grid=(steps_of(units),),
        in_specs=[tok, tokt, tok, tokt, w, w, wt], out_specs=[out, hid, hid],
        out_shape=[jax.ShapeDtypeStruct((3, 16, ff), BF)] + [jax.ShapeDtypeStruct((t, ff), BF)] * 2,
        scratch_shapes=[pltpu.VMEM((t, block), BF)] + exchange_scratch(units, block),
        compiler_params=sending(1), name="last", cost_estimate=cost(12 * t * d * ff, 4 * t * ff + 12 * d * ff),
    )(a, at, dy, dyt, w_gate, w_up, w_down)


def input_kernel(dg, du, wg, wu, h, dy, out, outt):
    da = (nt(dg[...], wg[0]).astype(BF).astype(F32) + nt(du[...], wu[0]).astype(BF).astype(F32)).astype(BF).astype(F32)
    wide = h[...].astype(F32)
    scale = lax.rsqrt(jnp.mean(wide * wide, -1, keepdims=True) + 1e-6)
    dot = jnp.mean(da * wide, -1, keepdims=True)
    dh = scale * da - wide * (scale * scale * scale * dot)
    o = dy[...].astype(F32) + dh.astype(BF).astype(F32)
    out[...] = o.astype(BF)
    outt[...] = o.astype(BF).T

def inputs(dg, du, w_gate, w_up, h, dy, number, block=512):
    t, d = h.shape
    ff = dg.shape[1]
    tok = pl.BlockSpec((block, d), lambda i: (i, 0))
    hid = pl.BlockSpec((block, ff), lambda i: (i, 0))
    w = pl.BlockSpec((1, d, ff), lambda i: (number, 0, 0), pipeline_mode=pl.Buffered(1))
    return pl.pallas_call(
        input_kernel, grid=(t // block,), in_specs=[hid, hid, w, w, tok, tok],
        out_specs=[tok, pl.BlockSpec((d, block), lambda i: (0, i))],
        out_shape=[jax.ShapeDtypeStruct((t, d), BF), jax.ShapeDtypeStruct((d, t), BF)],
        compiler_params=vmem(60), name="inputs", cost_estimate=cost(4 * t * d * ff, 4 * t * ff + 4 * d * ff),
    )(dg, du, w_gate, w_up, h, dy)

def first_kernel(units, at, dh, dht, wd, gate, up, out, act, dgs, dus, *scratch):
    k = pl.program_id(0)
    exchange(k, units, out, scratch)

    @pl.when(k < units)
    def _():
        for i in range(dh.shape[0] // TILE):
            da = nt(dh[rows(i)], wd[0]).astype(BF).astype(F32)
            c, dg, du = split(gate[rows(i)], up[rows(i)], da)
            act[rows(i)] = c.astype(BF)
            dgs[rows(i)] = dg.astype(BF)
            dus[rows(i)] = du.astype(BF)
        sums(k, units, scratch, ((dht, act), (at, dgs), (at, dus)))


def first(at, dh, dht, w_down, gate, up, number, block=256):
    t, d = dh.shape
    ff = gate.shape[1]
    units = pl.cdiv(ff, block)
    tok, tokt, _, wt, hid, out = specs(t, d, units, block, number)
    return pl.pallas_call(
        functools.partial(first_kernel, units), grid=(steps_of(units),),
        in_specs=[tokt, tok, tokt, wt, hid, hid], out_specs=out,
        out_shape=jax.ShapeDtypeStruct((3, 16, ff), BF),
        scratch_shapes=[pltpu.VMEM((t, block), BF)] * 3 + exchange_scratch(units, block),
        compiler_params=sending(2), name="first", cost_estimate=cost(8 * t * d * ff, 8 * t * ff + 8 * d * ff),
    )(at, dh, dht, w_down, gate, up)


def adamw_kernel(which, g, w, m, v, *refs):
    nw, nm, nv = refs[-3:]

    def part(at, grad):
        m2 = 0.9 * m[0, at] + 0.1 * grad
        v2 = 0.95 * v[0, at] + 0.05 * grad * grad
        wide = w[0, at].astype(F32)
        step = m2 * lax.rsqrt(v2 + 1e-8) + 0.1 * wide
        nw[0, at] = (wide - 0.02 * step).astype(BF)
        nm[0, at] = m2
        nv[0, at] = v2

    if which == 0:
        part(pl.ds(0, w.shape[1]), g[...].reshape(-1, g.shape[-1]).T.astype(F32))
    else:

        @pl.loop(0, 16)
        def _(i):
            a, b = lax.div(i, 4), lax.rem(i, 4)
            part(pl.ds(pl.multiple_of(i * 16, 16), 16), (g[b, 0, a, 0] if which == 1 else g[a, b, 0, 0]).astype(F32))


def adamw(which, g, w, m, v, number, before=None):
    _, r, c = w.shape
    block = 256 if which else 640
    spec = pl.BlockSpec((1, block, c), lambda i: (number, i, 0))
    gs = (
        pl.BlockSpec((4, 4, 4, 1, 16, block), lambda i: (0, 0, 0, 0, 0, i)),
        pl.BlockSpec((4, 1, 4, 1, 16, c), lambda i: (0, i, 0, 1, 0, 0)),
        pl.BlockSpec((4, 4, 1, 1, 16, c), lambda i: (0, 0, i, 2, 0, 0)),
    )[which]
    extra = [] if before is None else list(before)
    return pl.pallas_call(
        functools.partial(adamw_kernel, which), grid=(r // block,),
        in_specs=[gs, spec, spec, spec] + [pl.BlockSpec(memory_space=pl.ANY)] * len(extra),
        out_specs=[spec] * 3,
        out_shape=[jax.ShapeDtypeStruct(w.shape, BF), jax.ShapeDtypeStruct(w.shape, F32), jax.ShapeDtypeStruct(w.shape, F32)],
        input_output_aliases={4 + i: i for i in range(len(extra))},
        compiler_params=vmem(60), name="adamw", cost_estimate=cost(20 * r * c, 22 * r * c),
    )(g, w, m, v, *extra)


def gather(part):
    whole = lax.all_gather(part, "dp", axis=0, tiled=True)
    return whole.reshape(4, 4, 4, 3, 16, -1)


def solution(mesh):
    def step(x, dy, *arrays):
        (w_gate, w_up, w_down), moments, squares = (arrays[i : i + 3] for i in (0, 3, 6))
        x, dy = x[0], dy[0]
        a0, a0t, dyt = ready(x, dy)
        act, gate, up = gated(a0, w_gate, w_up, 0)
        h1, a1, a1t = down(act, w_down, x, 0)
        g1, dg, du = last(a1, a1t, dy, dyt, w_gate, w_up, w_down, 1)
        g1 = gather(g1)
        dh, dht = inputs(dg, du, w_gate, w_up, h1, dy, 1)
        g0 = gather(first(a0t, dh, dht, w_down, gate, up, 0))
        new = [None] * 3
        for number, g in ((1, g1), (0, g0)):
            for which, i in enumerate((2, 0, 1)):
                new[i] = adamw(which, g, arrays[i], moments[i], squares[i], number, new[i])
        return tuple(one[which] for which in range(3) for one in new)

    return jax.shard_map(
        step,
        mesh=mesh,
        in_specs=(P(("rep", "dp"), None, None),) * 2 + (P(None, None, None),) * 9,
        out_specs=(P("rep", None, None),) * 9,
        check_vma=False,
    )
```

time: 926 us -> 603 us (0.65)
  Pallas kernels: 0 us -> 549 us
  matrix products: 371 us -> 0 us
  waiting for transfers between devices: 369 us -> 40.3 us
  other arithmetic: 151 us -> 0 us
  local copies, waits for them, and re-layouts: 13 us -> 0 us
    pallas_call x0 -> x12, Pallas kernels: none -> 549 us  [the longest x1 151 us: first(): pl.pallas_call(functools.partial(first_kernel, units), grid=(steps_of(uni...]
    dot_general x15 -> x0, matrix products: 371 us -> none  [the longest x5 133 us: layer(): gate = jnp.dot(a, w['w_gate'], preferred_element_type=jnp.float32)]
    psum x1 -> x0, waiting for transfers between devices: 369 us -> none  [step(): summed[number] = [lax.psum(by_w[name], 'dp') for name in NAMES]]
    convert_element_type x2 -> x0, other arithmetic: 141 us -> none  [adamw(): return ((w - 0.02 * step).astype(jnp.bfloat16), m, v)]
    all_gather x0 -> x2, waiting for transfers between devices: none -> 40.3 us  [gather(): whole = lax.all_gather(part, 'dp', axis=0, tiled=True)]
    unnamed x18 -> x0, local copies, waits for them, and re-layouts: 13 us -> none
  transfers between devices with their start and end apart: 1 -> 2, of which waited for: 1 -> 1; matrix products, arithmetic and copies ran while one was open for 0% -> 0% of each run, Pallas kernels for 0% -> 44%
where the time goes in v1:
time: 603 us
  Pallas kernels  549 us (91%)
  waiting for transfers between devices  40.3 us (7%)
  between operations  14.1 us (2%)
    pallas_call x1, Pallas kernels, first(): pl.pallas_call(functools.partial(first_kernel, units), grid=(steps_of(uni...  151 us
    pallas_call x6, Pallas kernels, adamw(): pl.pallas_call(functools.partial(adamw_kernel, which), grid=(r // block,)...  147 us
    pallas_call x1, Pallas kernels, last(): pl.pallas_call(functools.partial(last_kernel, units), grid=(steps_of(unit...  139 us
    pallas_call x1, Pallas kernels, inputs(): pl.pallas_call(input_kernel, grid=(t // block,), in_specs=[hid, hid, w, w...  42 us
    all_gather x2, waiting for transfers between devices, gather(): whole = lax.all_gather(part, 'dp', axis=0, tiled=True)  40.3 us
    pallas_call x1, Pallas kernels, gated(): pl.pallas_call(gated_kernel, grid=(pl.cdiv(ff, block),), in_specs=[whole,...  35.4 us
    pallas_call x1, Pallas kernels, down(): pl.pallas_call(down_kernel, grid=(t // block,), in_specs=[pl.BlockSpec((b...  23.4 us
  transfers between devices with their start and end apart: 2, of which 1 were waited for; matrix products, arithmetic and copies ran while one was open for 0% of the time, Pallas kernels for 44%

profile of v1, /device:TPU:1, one launch (start us, length us, event | category | flops | bytes accessed | tf_op | source)
XLA Modules:
  0.0 603.1 jit_solution(749898456807009675)
XLA Ops:
  7.2 0.0 all-gather.5.cloned.1.call-start
  7.2 10.6 %ready.1 = (bf16[2048,1024]{1,0:T(8,128)(2,1)}, bf16[1024,2048]{1,0:T(8,128)(2,1)}, bf16[1024,2048]{1,0:T(8,128)(2,1)}) custom-call(bf16[2048,1024]{1,0:T(8,128)(2,1)} %bitcast.10, bf16[2048,1024]{1,0:T(8,128)(2,1)} %bitcast.12), custom_call_target="tpu_custom_call" | custom-call | flops 20971520 | bytes 20971520 | tf_op jit(solution)/shard_map/ready/pallas_call | solution.py:41
  17.8 35.4 %gated.1 = (bf16[2048,3200]{1,0:T(8,128)(2,1)}, f32[2048,3200]{1,0:T(8,128)}, f32[2048,3200]{1,0:T(8,128)}) custom-call(bf16[2048,1024]{1,0:T(8,128)(2,1)} %get-tuple-element.42.a, bf16[2,1024,3200]{2,1,0:T(8,128)(2,1)} %w.9, bf16[2,1024,3200]{2,1,0:T(8,128)(2,1)} %w.11), custom_call_target="tpu_custom_call" | custom-call | flops 26843545600 | bytes 78643200 | tf_op jit(solution)/shard_map/gated/pallas_call | solution.py:60
  53.3 23.4 %down.1 = (bf16[2048,1024]{1,0:T(8,128)(2,1)}, bf16[2048,1024]{1,0:T(8,128)(2,1)}, bf16[1024,2048]{1,0:T(8,128)(2,1)}) custom-call(bf16[2048,3200]{1,0:T(8,128)(2,1)} %get-tuple-element.43.act, bf16[2,3200,1024]{2,1,0:T(8,128)(2,1)} %w.13, bf16[2048,1024]{1,0:T(8,128)(2,1)} %bitcast.11), custom_call_target="tpu_custom_call" | custom-call | flops 13421772800 | bytes 19660800 | tf_op jit(solution)/shard_map/down/pallas_call | solution.py:80
  76.7 138.8 %last.1 = (bf16[3,16,3200]{2,1,0:T(8,128)(2,1)}, bf16[2048,3200]{1,0:T(8,128)(2,1)}, bf16[2048,3200]{1,0:T(8,128)(2,1)}) custom-call(bf16[2048,1024]{1,0:T(8,128)(2,1)} %get-tuple-element.44.a, bf16[1024,2048]{1,0:T(8,128)(2,1)} %get-tuple-element.45.at, bf16[2048,1024]{1,0:T(8,128)(2,1)} %bitcast.13, bf16[1024,2048]{1,0:T(8,128)(2,1)} %get-tuple-element.46.dyt, ...), custom_call_target="tpu_custom_call" | custom-call | flops 80530636800 | bytes 65536000 | tf_op jit(solution)/shard_map/last/pallas_call | solution.py:279
  215.5 0.0 all-gather.5.cloned.1.call-update
  215.5 0.0 all-gather.3.cloned.1.call-start
  215.6 42.0 %inputs.1 = (bf16[2048,1024]{1,0:T(8,128)(2,1)}, bf16[1024,2048]{1,0:T(8,128)(2,1)}) custom-call(bf16[2048,3200]{1,0:T(8,128)(2,1)} %get-tuple-element.47.dg, bf16[2048,3200]{1,0:T(8,128)(2,1)} %get-tuple-element.48.du, bf16[2,1024,3200]{2,1,0:T(8,128)(2,1)} %w.9, bf16[2,1024,3200]{2,1,0:T(8,128)(2,1)} %w.11, bf16[2048,1024]{1,0:T(8,128)(2,1)} %get-tuple-element.49.h, ...), custom_call_target="tpu_custom_call" | custom-call | flops 26843545600 | bytes 39321600 | tf_op jit(solution)/shard_map/inputs/pallas_call | solution.py:304
  257.5 151.2 %first.1 = bf16[3,16,3200]{2,1,0:T(8,128)(2,1)} custom-call(bf16[1024,2048]{1,0:T(8,128)(2,1)} %get-tuple-element.41.at, bf16[2048,1024]{1,0:T(8,128)(2,1)} %get-tuple-element.50.dh, bf16[1024,2048]{1,0:T(8,128)(2,1)} %get-tuple-element.51.dht, bf16[2,3200,1024]{2,1,0:T(8,128)(2,1)} %w.13, f32[2048,3200]{1,0:T(8,128)} %get-tuple-element.52.gate, ...), custom_call_target="tpu_custom_call" | custom-call | flops 53687091200 | bytes 78643200 | tf_op jit(solution)/shard_map/first/pallas_call | solution.py:331
  408.7 0.0 all-gather.3.cloned.1.call-update
  408.7 0.0 all-gather.5.cloned.1.call-done
  408.8 26.9 %adamw.10 = (bf16[2,3200,1024]{2,1,0:T(8,128)(2,1)}, f32[2,3200,1024]{2,1,0:T(8,128)}, f32[2,3200,1024]{2,1,0:T(8,128)}) custom-call(bf16[4,4,4,3,16,3200]{5,4,3,2,1,0:T(8,128)(2,1)} %bitcast.4, bf16[2,3200,1024]{2,1,0:T(8,128)(2,1)} %w.13, f32[2,3200,1024]{2,1,0:T(8,128)} %m.11, f32[2,3200,1024]{2,1,0:T(8,128)} %v.11), custom_call_target="tpu_custom_call" | custom-call | flops 65536000 | bytes 72089600 | tf_op jit(solution)/shard_map/adamw/pallas_call | solution.py:372
  435.7 23.4 %adamw.8 = (bf16[2,1024,3200]{2,1,0:T(8,128)(2,1)}, f32[2,1024,3200]{2,1,0:T(8,128)}, f32[2,1024,3200]{2,1,0:T(8,128)}) custom-call(bf16[4,4,4,3,16,3200]{5,4,3,2,1,0:T(8,128)(2,1)} %bitcast.5, bf16[2,1024,3200]{2,1,0:T(8,128)(2,1)} %w.11, f32[2,1024,3200]{2,1,0:T(8,128)} %m.9, f32[2,1024,3200]{2,1,0:T(8,128)} %v.9), custom_call_target="tpu_custom_call" | custom-call | flops 65536000 | bytes 72089600 | tf_op jit(solution)/shard_map/adamw/pallas_call | solution.py:372
  459.1 23.4 %adamw.6 = (bf16[2,1024,3200]{2,1,0:T(8,128)(2,1)}, f32[2,1024,3200]{2,1,0:T(8,128)}, f32[2,1024,3200]{2,1,0:T(8,128)}) custom-call(bf16[4,4,4,3,16,3200]{5,4,3,2,1,0:T(8,128)(2,1)} %bitcast.6, bf16[2,1024,3200]{2,1,0:T(8,128)(2,1)} %w.9, f32[2,1024,3200]{2,1,0:T(8,128)} %m.7, f32[2,1024,3200]{2,1,0:T(8,128)} %v.7), custom_call_target="tpu_custom_call" | custom-call | flops 65536000 | bytes 72089600 | tf_op jit(solution)/shard_map/adamw/pallas_call | solution.py:372
  482.5 40.3 %all-gather.3.cloned.1.call-done = bf16[192,16,3200]{2,1,0:T(8,128)(2,1)} async-done(((bf16[3,16,3200]{2,1,0:T(8,128)(2,1)}), bf16[192,16,3200]{2,1,0:T(8,128)(2,1)}) %all-gather.3.cloned.1.call-update) | async-done | bytes 19660816 | tf_op jit(solution)/shard_map/all_gather | solution.py:383
  522.8 26.7 %adamw.11 = (bf16[2,3200,1024]{2,1,0:T(8,128)(2,1)}, f32[2,3200,1024]{2,1,0:T(8,128)}, f32[2,3200,1024]{2,1,0:T(8,128)}) custom-call(bf16[4,4,4,3,16,3200]{5,4,3,2,1,0:T(8,128)(2,1)} %bitcast.7, bf16[2,3200,1024]{2,1,0:T(8,128)(2,1)} %w.13, f32[2,3200,1024]{2,1,0:T(8,128)} %m.11, ...), custom_call_target="tpu_custom_call", output_to_operand_aliasing={{0}: (4, {}), {1}: (5, {}), {2}: (6, {})} | custom-call | flops 65536000 | bytes 72089600 | tf_op jit(solution)/shard_map/adamw/pallas_call | solution.py:372
  549.5 23.4 %adamw.9 = (bf16[2,1024,3200]{2,1,0:T(8,128)(2,1)}, f32[2,1024,3200]{2,1,0:T(8,128)}, f32[2,1024,3200]{2,1,0:T(8,128)}) custom-call(bf16[4,4,4,3,16,3200]{5,4,3,2,1,0:T(8,128)(2,1)} %bitcast.8, bf16[2,1024,3200]{2,1,0:T(8,128)(2,1)} %w.11, f32[2,1024,3200]{2,1,0:T(8,128)} %m.9, ...), custom_call_target="tpu_custom_call", output_to_operand_aliasing={{0}: (4, {}), {1}: (5, {}), {2}: (6, {})} | custom-call | flops 65536000 | bytes 72089600 | tf_op jit(solution)/shard_map/adamw/pallas_call | solution.py:372
  572.9 23.4 %adamw.7 = (bf16[2,1024,3200]{2,1,0:T(8,128)(2,1)}, f32[2,1024,3200]{2,1,0:T(8,128)}, f32[2,1024,3200]{2,1,0:T(8,128)}) custom-call(bf16[4,4,4,3,16,3200]{5,4,3,2,1,0:T(8,128)(2,1)} %bitcast.9, bf16[2,1024,3200]{2,1,0:T(8,128)(2,1)} %w.9, f32[2,1024,3200]{2,1,0:T(8,128)} %m.7, ...), custom_call_target="tpu_custom_call", output_to_operand_aliasing={{0}: (4, {}), {1}: (5, {}), {2}: (6, {})} | custom-call | flops 65536000 | bytes 72089600 | tf_op jit(solution)/shard_map/adamw/pallas_call | solution.py:372
Async XLA Ops:
  7.2 401.6 %all-gather.5.cloned.1.call-start = ((), (), s32[]{:S(2)}) async-start(), calls=%async_computation.1 | async-start | bytes 19968000 | tf_op jit(solution)/shard_map/all_gather | solution.py:383
  215.5 307.3 %all-gather.3.cloned.1.call-start = ((), (), s32[]{:S(2)}) async-start(), calls=%async_computation | async-start | bytes 19968000 | tf_op jit(solution)/shard_map/all_gather | solution.py:383
Sparse Core Ops, SparseCore 0:
  215.6 163.8 all-gather.4
  408.9 113.8 all-gather.2

commit v2 on v1

--- a/solution.py
+++ b/solution.py
@@ -27,59 +27,66 @@
 def sig(x):
     return 1.0 / (1.0 + jnp.exp(-x))
 
-def ready_kernel(x, dy, a, at, dyt):
+def ready_kernel(x, a):
     wide = x[...].astype(F32)
-    n = wide * lax.rsqrt(jnp.mean(wide * wide, -1, keepdims=True) + 1e-6)
-    a[...] = n.astype(BF)
-    at[...] = n.astype(BF).T
-    dyt[...] = dy[...].T
-
-def ready(x, dy, block=256):
+    a[...] = (wide * lax.rsqrt(jnp.mean(wide * wide, -1, keepdims=True) + 1e-6)).astype(BF)
+
+
+def ready(x, block=512):
     t, d = x.shape
     tok = pl.BlockSpec((block, d), lambda i: (i, 0))
-    tokt = pl.BlockSpec((d, block), lambda i: (0, i))
-    return pl.pallas_call(
-        ready_kernel, grid=(t // block,), in_specs=[tok, tok], out_specs=[tok, tokt, tokt],
-        out_shape=[jax.ShapeDtypeStruct((t, d), BF)] + [jax.ShapeDtypeStruct((d, t), BF)] * 2,
-        compiler_params=vmem(60), name="ready", cost_estimate=cost(10 * t * d, 10 * t * d),
-    )(x, dy)
-
-def gated_kernel(a, wg, wu, act, gate, up):
+    return pl.pallas_call(
+        ready_kernel, grid=(t // block,), in_specs=[tok], out_specs=tok, out_shape=jax.ShapeDtypeStruct((t, d), BF),
+        compiler_params=vmem(60), name="ready", cost_estimate=cost(5 * t * d, 4 * t * d),
+    )(x)
+
+
+def gated_kernel(a, wg, wu, dy, act, gate, up, at, dyt):
+    n = at.shape[1]
+    start = jnp.minimum(pl.program_id(0), a.shape[0] // n - 1) * n
+    dyt[...] = dy[...].T
+    at[...] = a[pl.ds(pl.multiple_of(start, n), n)].T
     for i in range(a.shape[0] // TILE):
         g, u = nn(a[rows(i)], wg[0]), nn(a[rows(i)], wu[0])
         gate[rows(i)] = g
         up[rows(i)] = u
         act[rows(i)] = (g * sig(g) * u).astype(BF)
 
-def gated(a, w_gate, w_up, number, block=256):
+
+def gated(a, dy, w_gate, w_up, number, block=256, tokens=256):
     t, d = a.shape
     ff = w_gate.shape[2]
-    whole = pl.BlockSpec((t, d), lambda j: (0, 0))
+    whole = pl.BlockSpec((t, d), lambda j: (0, 0), pipeline_mode=pl.Buffered(1))
     w = pl.BlockSpec((1, d, block), lambda j: (number, 0, j))
     out = pl.BlockSpec((t, block), lambda j: (0, j))
-    return pl.pallas_call(
-        gated_kernel, grid=(pl.cdiv(ff, block),), in_specs=[whole, w, w], out_specs=[out] * 3,
-        out_shape=[jax.ShapeDtypeStruct((t, ff), x) for x in (BF, F32, F32)],
+    turned = pl.BlockSpec((d, tokens), lambda j: (0, jnp.minimum(j, t // tokens - 1)))
+    return pl.pallas_call(
+        gated_kernel, grid=(pl.cdiv(ff, block),),
+        in_specs=[whole, w, w, pl.BlockSpec((tokens, d), lambda j: (jnp.minimum(j, t // tokens - 1), 0))],
+        out_specs=[out] * 3 + [turned] * 2,
+        out_shape=[jax.ShapeDtypeStruct((t, ff), x) for x in (BF, F32, F32)] + [jax.ShapeDtypeStruct((d, t), BF)] * 2,
         compiler_params=vmem(60), name="gated", cost_estimate=cost(4 * t * d * ff, 10 * t * ff + 4 * d * ff),
-    )(a, w_gate, w_up)
-
-def down_kernel(act, w, h, out, a, at):
-    o = h[...].astype(F32) + nn(act[...], w[0]).astype(BF).astype(F32)
-    o = o.astype(BF)
-    out[...] = o
-    wide = o.astype(F32)
-    scale = lax.rsqrt(jnp.mean(wide * wide, -1, keepdims=True) + 1e-6)
-    n = wide * scale
-    a[...] = n.astype(BF)
-    at[...] = n.astype(BF).T
-
-def down(act, w_down, h, number, block=512):
+    )(a, w_gate, w_up, dy)
+
+
+def down_kernel(sub, act, w, h, out, a, at):
+    for i in range(act.shape[0] // sub):
+        r = pl.ds(i * sub, sub)
+        o = (h[r].astype(F32) + nn(act[r], w[0]).astype(BF).astype(F32)).astype(BF)
+        out[r] = o
+        wide = o.astype(F32)
+        n = (wide * lax.rsqrt(jnp.mean(wide * wide, -1, keepdims=True) + 1e-6)).astype(BF)
+        a[r] = n
+        at[:, r] = n.T
+
+
+def down(act, w_down, h, number, block=512, sub=256):
     t, d = h.shape
     ff = act.shape[1]
     tok = pl.BlockSpec((block, d), lambda i: (i, 0))
     return pl.pallas_call(
-        down_kernel, grid=(t // block,),
-        in_specs=[pl.BlockSpec((block, ff), lambda i: (i, 0)), pl.BlockSpec((1, ff, d), lambda i: (number, 0, 0)), tok],
+        functools.partial(down_kernel, sub), grid=(t // block,),
+        in_specs=[pl.BlockSpec((block, ff), lambda i: (i, 0)), pl.BlockSpec((1, ff, d), lambda i: (number, 0, 0), pipeline_mode=pl.Buffered(1)), tok],
         out_specs=[tok, tok, pl.BlockSpec((d, block), lambda i: (0, i))],
         out_shape=[jax.ShapeDtypeStruct((t, d), BF)] * 2 + [jax.ShapeDtypeStruct((d, t), BF)],
         compiler_params=vmem(60), name="down", cost_estimate=cost(2 * t * d * ff, 2 * t * ff + 2 * d * ff),
@@ -90,13 +97,12 @@
     silu = g * s
     return (silu * u), da * u * (s + silu * (1.0 - s)), da * silu
 
-LAG = 2
 STAGES = 5
 STRIDE = (16, 4, 1)
 
 
-def exchange_scratch(units, block):
-    local, kept = 2 * LAG + 1, LAG + 1
+def exchange_scratch(units, block, lag):
+    local, kept = 2 * lag + 1, lag + 1
     return [
         pltpu.VMEM((3, local, 1152, block), BF),
         pltpu.VMEM((3, units, 2, 256, block), BF),
@@ -113,13 +119,13 @@
     ]
 
 
-def steps_of(units):
-    return units + 1 + STAGES * LAG
-
-
-def exchange(k, units, out, scratch):
+def steps_of(units, lag):
+    return units + 1 + STAGES * lag
+
+
+def exchange(k, units, lag, out, scratch):
     term, in0, in1, one, one_b, in2, in3, two, two_b, in4, sent, got = scratch
-    local, kept = 2 * LAG + 1, LAG + 1
+    local, kept = 2 * lag + 1, lag + 1
     me = lax.axis_index("dp")
     at = (lax.div(me, 16), lax.rem(lax.div(me, 4), 4), lax.rem(me, 4))
 
@@ -212,7 +218,7 @@
                 out[c] = s.astype(BF)
 
     for stage in range(STAGES + 1):
-        u = k - 1 - stage * LAG
+        u = k - 1 - stage * lag
 
         @pl.when((u >= 0) & (u < units))
         def _(stage=stage, u=u):
@@ -231,15 +237,15 @@
         term[c, slot, pl.ds(1024, 128)] = value[:128]
 
 
-def sums(k, units, scratch, pairs):
+def sums(k, lag, scratch, pairs):
     for i in range(pairs[0][0].shape[0] // TILE):
         for c, (left, right) in enumerate(pairs):
-            keep(scratch[0], c, lax.rem(k, 2 * LAG + 1), i, nn(left[rows(i)], right[...]).astype(BF))
-
-
-def last_kernel(units, a, at, dy, dyt, wg, wu, wd, out, dg_out, du_out, act, *scratch):
+            keep(scratch[0], c, lax.rem(k, 2 * lag + 1), i, nn(left[rows(i)], right[...]).astype(BF))
+
+
+def last_kernel(units, lag, a, at, dy, dyt, wg, wu, wd, out, dg_out, du_out, act, *scratch):
     k = pl.program_id(0)
-    exchange(k, units, out, scratch)
+    exchange(k, units, lag, out, scratch)
 
     @pl.when(k < units)
     def _():
@@ -249,10 +255,10 @@
             act[rows(i)] = c.astype(BF)
             dg_out[rows(i)] = dg.astype(BF)
             du_out[rows(i)] = du.astype(BF)
-        sums(k, units, scratch, ((dyt, act), (at, dg_out), (at, du_out)))
-
-
-def specs(t, d, units, block, number):
+        sums(k, lag, scratch, ((dyt, act), (at, dg_out), (at, du_out)))
+
+
+def specs(t, d, units, lag, block, number):
     def j(k):
         return jnp.minimum(k, units - 1)
 
@@ -263,7 +269,7 @@
         pl.BlockSpec((1, d, block), lambda k: (number, 0, j(k))),
         pl.BlockSpec((1, block, d), lambda k: (number, j(k), 0)),
         pl.BlockSpec((t, block), lambda k: (0, j(k))),
-        pl.BlockSpec((3, 16, block), lambda k: (0, 0, jnp.clip(k - 1 - STAGES * LAG, 0, units - 1))),
+        pl.BlockSpec((3, 16, block), lambda k: (0, 0, jnp.clip(k - 1 - STAGES * lag, 0, units - 1))),
     )
 
 
@@ -271,46 +277,49 @@
     return pltpu.CompilerParams(vmem_limit_bytes=63 << 20, dimension_semantics=("arbitrary",), collective_id=number, has_side_effects=True)
 
 
-def last(a, at, dy, dyt, w_gate, w_up, w_down, number, block=256):
+def last(a, at, dy, dyt, w_gate, w_up, w_down, number, block=256, lag=1):
     t, d = a.shape
     ff = w_gate.shape[2]
     units = pl.cdiv(ff, block)
-    tok, tokt, w, wt, hid, out = specs(t, d, units, block, number)
-    return pl.pallas_call(
-        functools.partial(last_kernel, units), grid=(steps_of(units),),
+    tok, tokt, w, wt, hid, out = specs(t, d, units, lag, block, number)
+    return pl.pallas_call(
+        functools.partial(last_kernel, units, lag), grid=(steps_of(units, lag),),
         in_specs=[tok, tokt, tok, tokt, w, w, wt], out_specs=[out, hid, hid],
         out_shape=[jax.ShapeDtypeStruct((3, 16, ff), BF)] + [jax.ShapeDtypeStruct((t, ff), BF)] * 2,
-        scratch_shapes=[pltpu.VMEM((t, block), BF)] + exchange_scratch(units, block),
+        scratch_shapes=[pltpu.VMEM((t, block), BF)] + exchange_scratch(units, block, lag),
         compiler_params=sending(1), name="last", cost_estimate=cost(12 * t * d * ff, 4 * t * ff + 12 * d * ff),
     )(a, at, dy, dyt, w_gate, w_up, w_down)
 
 
-def input_kernel(dg, du, wg, wu, h, dy, out, outt):
-    da = (nt(dg[...], wg[0]).astype(BF).astype(F32) + nt(du[...], wu[0]).astype(BF).astype(F32)).astype(BF).astype(F32)
-    wide = h[...].astype(F32)
-    scale = lax.rsqrt(jnp.mean(wide * wide, -1, keepdims=True) + 1e-6)
-    dot = jnp.mean(da * wide, -1, keepdims=True)
-    dh = scale * da - wide * (scale * scale * scale * dot)
-    o = dy[...].astype(F32) + dh.astype(BF).astype(F32)
-    out[...] = o.astype(BF)
-    outt[...] = o.astype(BF).T
-
-def inputs(dg, du, w_gate, w_up, h, dy, number, block=512):
+def input_kernel(sub, dg, du, wg, wu, h, dy, out, outt):
+    for i in range(dg.shape[0] // sub):
+        r = pl.ds(i * sub, sub)
+        da = (nt(dg[r], wg[0]).astype(BF).astype(F32) + nt(du[r], wu[0]).astype(BF).astype(F32)).astype(BF).astype(F32)
+        wide = h[r].astype(F32)
+        scale = lax.rsqrt(jnp.mean(wide * wide, -1, keepdims=True) + 1e-6)
+        dot = jnp.mean(da * wide, -1, keepdims=True)
+        dh = scale * da - wide * (scale * scale * scale * dot)
+        o = (dy[r].astype(F32) + dh.astype(BF).astype(F32)).astype(BF)
+        out[r] = o
+        outt[:, r] = o.T
+
+
+def inputs(dg, du, w_gate, w_up, h, dy, number, block=512, sub=256):
     t, d = h.shape
     ff = dg.shape[1]
     tok = pl.BlockSpec((block, d), lambda i: (i, 0))
     hid = pl.BlockSpec((block, ff), lambda i: (i, 0))
     w = pl.BlockSpec((1, d, ff), lambda i: (number, 0, 0), pipeline_mode=pl.Buffered(1))
     return pl.pallas_call(
-        input_kernel, grid=(t // block,), in_specs=[hid, hid, w, w, tok, tok],
+        functools.partial(input_kernel, sub), grid=(t // block,), in_specs=[hid, hid, w, w, tok, tok],
         out_specs=[tok, pl.BlockSpec((d, block), lambda i: (0, i))],
         out_shape=[jax.ShapeDtypeStruct((t, d), BF), jax.ShapeDtypeStruct((d, t), BF)],
         compiler_params=vmem(60), name="inputs", cost_estimate=cost(4 * t * d * ff, 4 * t * ff + 4 * d * ff),
     )(dg, du, w_gate, w_up, h, dy)
 
-def first_kernel(units, at, dh, dht, wd, gate, up, out, act, dgs, dus, *scratch):
+def first_kernel(units, lag, at, dh, dht, wd, gate, up, out, act, dgs, dus, *scratch):
     k = pl.program_id(0)
-    exchange(k, units, out, scratch)
+    exchange(k, units, lag, out, scratch)
 
     @pl.when(k < units)
     def _():
@@ -320,19 +329,19 @@
             act[rows(i)] = c.astype(BF)
             dgs[rows(i)] = dg.astype(BF)
             dus[rows(i)] = du.astype(BF)
-        sums(k, units, scratch, ((dht, act), (at, dgs), (at, dus)))
-
-
-def first(at, dh, dht, w_down, gate, up, number, block=256):
+        sums(k, lag, scratch, ((dht, act), (at, dgs), (at, dus)))
+
+
+def first(at, dh, dht, w_down, gate, up, number, block=256, lag=2):
     t, d = dh.shape
     ff = gate.shape[1]
     units = pl.cdiv(ff, block)
-    tok, tokt, _, wt, hid, out = specs(t, d, units, block, number)
-    return pl.pallas_call(
-        functools.partial(first_kernel, units), grid=(steps_of(units),),
+    tok, tokt, _, wt, hid, out = specs(t, d, units, lag, block, number)
+    return pl.pallas_call(
+        functools.partial(first_kernel, units, lag), grid=(steps_of(units, lag),),
         in_specs=[tokt, tok, tokt, wt, hid, hid], out_specs=out,
         out_shape=jax.ShapeDtypeStruct((3, 16, ff), BF),
-        scratch_shapes=[pltpu.VMEM((t, block), BF)] * 3 + exchange_scratch(units, block),
+        scratch_shapes=[pltpu.VMEM((t, block), BF)] * 3 + exchange_scratch(units, block, lag),
         compiler_params=sending(2), name="first", cost_estimate=cost(8 * t * d * ff, 8 * t * ff + 8 * d * ff),
     )(at, dh, dht, w_down, gate, up)
 
@@ -388,8 +397,7 @@
     def step(x, dy, *arrays):
         (w_gate, w_up, w_down), moments, squares = (arrays[i : i + 3] for i in (0, 3, 6))
         x, dy = x[0], dy[0]
-        a0, a0t, dyt = ready(x, dy)
-        act, gate, up = gated(a0, w_gate, w_up, 0)
+        act, gate, up, a0t, dyt = gated(ready(x), dy, w_gate, w_up, 0)
         h1, a1, a1t = down(act, w_down, x, 0)
         g1, dg, du = last(a1, a1t, dy, dyt, w_gate, w_up, w_down, 1)
         g1 = gather(g1)

time: 603 us -> 596 us (0.988)
  Pallas kernels: 549 us -> 542 us
    pallas_call x5, Pallas kernels: 366 us -> 357 us  [the longest x1 151 us: first(): pl.pallas_call(functools.partial(first_kernel, units, lag), grid=(steps_o...]
  transfers between devices with their start and end apart: 2 -> 2, of which waited for: 1 -> 1; matrix products, arithmetic and copies ran while one was open for 0% -> 0% of each run, Pallas kernels for 44% -> 45%
where the time goes in v2:
time: 596 us
  Pallas kernels  542 us (91%)
  waiting for transfers between devices  40.1 us (7%)
  between operations  14.1 us (2%)
    pallas_call x1, Pallas kernels, first(): pl.pallas_call(functools.partial(first_kernel, units, lag), grid=(steps_o...  151 us
    pallas_call x6, Pallas kernels, adamw(): pl.pallas_call(functools.partial(adamw_kernel, which), grid=(r // block,)...  147 us
    pallas_call x1, Pallas kernels, last(): pl.pallas_call(functools.partial(last_kernel, units, lag), grid=(steps_of...  137 us
    pallas_call x1, Pallas kernels, inputs(): pl.pallas_call(functools.partial(input_kernel, sub), grid=(t // block,),...  40.8 us
    all_gather x2, waiting for transfers between devices, gather(): whole = lax.all_gather(part, 'dp', axis=0, tiled=True)  40.1 us
    pallas_call x1, Pallas kernels, gated(): pl.pallas_call(gated_kernel, grid=(pl.cdiv(ff, block),), in_specs=[whole,...  37.1 us
    pallas_call x1, Pallas kernels, down(): pl.pallas_call(functools.partial(down_kernel, sub), grid=(t // block,), i...  23.1 us
  transfers between devices with their start and end apart: 2, of which 1 were waited for; matrix products, arithmetic and copies ran while one was open for 0% of the time, Pallas kernels for 45%

profile of v2, /device:TPU:1, one launch (start us, length us, event | category | flops | bytes accessed | tf_op | source)
XLA Modules:
  0.0 595.9 jit_solution(12439245455677267488)
XLA Ops:
  7.2 0.0 all-gather.5.cloned.1.call-start
  7.2 5.2 ready.1.a
  12.4 37.1 %gated.1 = (bf16[2048,3200]{1,0:T(8,128)(2,1)}, f32[2048,3200]{1,0:T(8,128)}, f32[2048,3200]{1,0:T(8,128)}, bf16[1024,2048]{1,0:T(8,128)(2,1)}, bf16[1024,2048]{1,0:T(8,128)(2,1)}) custom-call(bf16[2048,1024]{1,0:T(8,128)(2,1)} %ready.1.a, bf16[2,1024,3200]{2,1,0:T(8,128)(2,1)} %w.9, bf16[2,1024,3200]{2,1,0:T(8,128)(2,1)} %w.11, bf16[2048,1024]{1,0:T(8,128)(2,1)} %bitcast.12), custom_call_target="tpu_custom_call" | custom-call | flops 26843545600 | bytes 78643200 | tf_op jit(solution)/shard_map/gated/pallas_call | solution.py:63
  49.5 23.1 %down.1 = (bf16[2048,1024]{1,0:T(8,128)(2,1)}, bf16[2048,1024]{1,0:T(8,128)(2,1)}, bf16[1024,2048]{1,0:T(8,128)(2,1)}) custom-call(bf16[2048,3200]{1,0:T(8,128)(2,1)} %get-tuple-element.41.act, bf16[2,3200,1024]{2,1,0:T(8,128)(2,1)} %w.13, bf16[2048,1024]{1,0:T(8,128)(2,1)} %bitcast.11), custom_call_target="tpu_custom_call" | custom-call | flops 13421772800 | bytes 19660800 | tf_op jit(solution)/shard_map/down/pallas_call | solution.py:87
  72.6 136.9 %last.1 = (bf16[3,16,3200]{2,1,0:T(8,128)(2,1)}, bf16[2048,3200]{1,0:T(8,128)(2,1)}, bf16[2048,3200]{1,0:T(8,128)(2,1)}) custom-call(bf16[2048,1024]{1,0:T(8,128)(2,1)} %get-tuple-element.42.a, bf16[1024,2048]{1,0:T(8,128)(2,1)} %get-tuple-element.43.at, bf16[2048,1024]{1,0:T(8,128)(2,1)} %bitcast.13, bf16[1024,2048]{1,0:T(8,128)(2,1)} %get-tuple-element.44.dyt, ...), custom_call_target="tpu_custom_call" | custom-call | flops 80530636800 | bytes 65536000 | tf_op jit(solution)/shard_map/last/pallas_call | solution.py:285
  209.6 0.0 all-gather.5.cloned.1.call-update
  209.6 0.0 all-gather.3.cloned.1.call-start
  209.6 40.8 %inputs.1 = (bf16[2048,1024]{1,0:T(8,128)(2,1)}, bf16[1024,2048]{1,0:T(8,128)(2,1)}) custom-call(bf16[2048,3200]{1,0:T(8,128)(2,1)} %get-tuple-element.45.dg, bf16[2048,3200]{1,0:T(8,128)(2,1)} %get-tuple-element.46.du, bf16[2,1024,3200]{2,1,0:T(8,128)(2,1)} %w.9, bf16[2,1024,3200]{2,1,0:T(8,128)(2,1)} %w.11, bf16[2048,1024]{1,0:T(8,128)(2,1)} %get-tuple-element.47.h, ...), custom_call_target="tpu_custom_call" | custom-call | flops 26843545600 | bytes 39321600 | tf_op jit(solution)/shard_map/inputs/pallas_call | solution.py:313
  250.5 151.4 %first.1 = bf16[3,16,3200]{2,1,0:T(8,128)(2,1)} custom-call(bf16[1024,2048]{1,0:T(8,128)(2,1)} %get-tuple-element.40.at, bf16[2048,1024]{1,0:T(8,128)(2,1)} %get-tuple-element.48.dh, bf16[1024,2048]{1,0:T(8,128)(2,1)} %get-tuple-element.49.dht, bf16[2,3200,1024]{2,1,0:T(8,128)(2,1)} %w.13, f32[2048,3200]{1,0:T(8,128)} %get-tuple-element.50.gate, ...), custom_call_target="tpu_custom_call" | custom-call | flops 53687091200 | bytes 78643200 | tf_op jit(solution)/shard_map/first/pallas_call | solution.py:340
  401.9 0.0 all-gather.3.cloned.1.call-update
  401.9 0.0 all-gather.5.cloned.1.call-done
  402.0 26.7 %adamw.10 = (bf16[2,3200,1024]{2,1,0:T(8,128)(2,1)}, f32[2,3200,1024]{2,1,0:T(8,128)}, f32[2,3200,1024]{2,1,0:T(8,128)}) custom-call(bf16[4,4,4,3,16,3200]{5,4,3,2,1,0:T(8,128)(2,1)} %bitcast.4, bf16[2,3200,1024]{2,1,0:T(8,128)(2,1)} %w.13, f32[2,3200,1024]{2,1,0:T(8,128)} %m.11, f32[2,3200,1024]{2,1,0:T(8,128)} %v.11), custom_call_target="tpu_custom_call" | custom-call | flops 65536000 | bytes 72089600 | tf_op jit(solution)/shard_map/adamw/pallas_call | solution.py:381
  428.7 23.4 %adamw.8 = (bf16[2,1024,3200]{2,1,0:T(8,128)(2,1)}, f32[2,1024,3200]{2,1,0:T(8,128)}, f32[2,1024,3200]{2,1,0:T(8,128)}) custom-call(bf16[4,4,4,3,16,3200]{5,4,3,2,1,0:T(8,128)(2,1)} %bitcast.5, bf16[2,1024,3200]{2,1,0:T(8,128)(2,1)} %w.11, f32[2,1024,3200]{2,1,0:T(8,128)} %m.9, f32[2,1024,3200]{2,1,0:T(8,128)} %v.9), custom_call_target="tpu_custom_call" | custom-call | flops 65536000 | bytes 72089600 | tf_op jit(solution)/shard_map/adamw/pallas_call | solution.py:381
  452.1 23.4 %adamw.6 = (bf16[2,1024,3200]{2,1,0:T(8,128)(2,1)}, f32[2,1024,3200]{2,1,0:T(8,128)}, f32[2,1024,3200]{2,1,0:T(8,128)}) custom-call(bf16[4,4,4,3,16,3200]{5,4,3,2,1,0:T(8,128)(2,1)} %bitcast.6, bf16[2,1024,3200]{2,1,0:T(8,128)(2,1)} %w.9, f32[2,1024,3200]{2,1,0:T(8,128)} %m.7, f32[2,1024,3200]{2,1,0:T(8,128)} %v.7), custom_call_target="tpu_custom_call" | custom-call | flops 65536000 | bytes 72089600 | tf_op jit(solution)/shard_map/adamw/pallas_call | solution.py:381
  475.5 40.1 %all-gather.3.cloned.1.call-done = bf16[192,16,3200]{2,1,0:T(8,128)(2,1)} async-done(((bf16[3,16,3200]{2,1,0:T(8,128)(2,1)}), bf16[192,16,3200]{2,1,0:T(8,128)(2,1)}) %all-gather.3.cloned.1.call-update) | async-done | bytes 19660816 | tf_op jit(solution)/shard_map/all_gather | solution.py:392
  515.6 26.7 %adamw.11 = (bf16[2,3200,1024]{2,1,0:T(8,128)(2,1)}, f32[2,3200,1024]{2,1,0:T(8,128)}, f32[2,3200,1024]{2,1,0:T(8,128)}) custom-call(bf16[4,4,4,3,16,3200]{5,4,3,2,1,0:T(8,128)(2,1)} %bitcast.7, bf16[2,3200,1024]{2,1,0:T(8,128)(2,1)} %w.13, f32[2,3200,1024]{2,1,0:T(8,128)} %m.11, ...), custom_call_target="tpu_custom_call", output_to_operand_aliasing={{0}: (4, {}), {1}: (5, {}), {2}: (6, {})} | custom-call | flops 65536000 | bytes 72089600 | tf_op jit(solution)/shard_map/adamw/pallas_call | solution.py:381
  542.2 23.4 %adamw.9 = (bf16[2,1024,3200]{2,1,0:T(8,128)(2,1)}, f32[2,1024,3200]{2,1,0:T(8,128)}, f32[2,1024,3200]{2,1,0:T(8,128)}) custom-call(bf16[4,4,4,3,16,3200]{5,4,3,2,1,0:T(8,128)(2,1)} %bitcast.8, bf16[2,1024,3200]{2,1,0:T(8,128)(2,1)} %w.11, f32[2,1024,3200]{2,1,0:T(8,128)} %m.9, ...), custom_call_target="tpu_custom_call", output_to_operand_aliasing={{0}: (4, {}), {1}: (5, {}), {2}: (6, {})} | custom-call | flops 65536000 | bytes 72089600 | tf_op jit(solution)/shard_map/adamw/pallas_call | solution.py:381
  565.6 23.4 %adamw.7 = (bf16[2,1024,3200]{2,1,0:T(8,128)(2,1)}, f32[2,1024,3200]{2,1,0:T(8,128)}, f32[2,1024,3200]{2,1,0:T(8,128)}) custom-call(bf16[4,4,4,3,16,3200]{5,4,3,2,1,0:T(8,128)(2,1)} %bitcast.9, bf16[2,1024,3200]{2,1,0:T(8,128)(2,1)} %w.9, f32[2,1024,3200]{2,1,0:T(8,128)} %m.7, ...), custom_call_target="tpu_custom_call", output_to_operand_aliasing={{0}: (4, {}), {1}: (5, {}), {2}: (6, {})} | custom-call | flops 65536000 | bytes 72089600 | tf_op jit(solution)/shard_map/adamw/pallas_call | solution.py:381
Async XLA Ops:
  7.2 394.8 %all-gather.5.cloned.1.call-start = ((), (), s32[]{:S(2)}) async-start(), calls=%async_computation.1 | async-start | bytes 19968000 | tf_op jit(solution)/shard_map/all_gather | solution.py:392
  209.6 306.0 %all-gather.3.cloned.1.call-start = ((), (), s32[]{:S(2)}) async-start(), calls=%async_computation | async-start | bytes 19968000 | tf_op jit(solution)/shard_map/all_gather | solution.py:392
Sparse Core Ops, SparseCore 0:
  209.7 166.0 all-gather.4
  402.1 113.4 all-gather.2
